TPU v7x, 32 devices: a whole 2x2x4 slice. The times are simulated.
32 devices in a mesh: head: 4 (over x, core), ctx: 8 (over z, y).
Axes of the slice: x: 2, y: 2, z: 4, core: 2. Of those that a mesh axis runs over, the one named last changes fastest.
Arguments:
- token_ids: int32 [2, 16], replicated, may hold values from 0 to 64127
- suffix_lengths: int32 [16], replicated, may hold values from 0 to 128, as said below
- embedding: bfloat16 [64128, 16384], P('ctx', 'head'), may hold values from -36 to 36
- attn_gain: float32 [16384], P('head'), may hold values from 0.25 to 1.75
- qkv_weight: bfloat16 [16384, 8, 1280], P('head', None, 'ctx'), may hold values from -0.046875 to 0.046875
- out_weight: bfloat16 [8192, 16384], P('head', 'ctx'), may hold values from -0.0625 to 0.0625
- prefix_keys: bfloat16 [8, 32768, 128], P('head', 'ctx'), may hold values from -32 to 32
- prefix_values: bfloat16 [8, 32768, 128], P('head', 'ctx'), may hold values from -8 to 8
- suffix_keys: bfloat16 [16, 128, 8, 128], P('ctx', None, 'head'), may hold values from -32 to 32
- suffix_values: bfloat16 [16, 128, 8, 128], P('ctx', None, 'head'), may hold values from -12 to 12
Outputs:
- attn_out: bfloat16 [16, 2, 16384], P('head', None, 'ctx')
Inputs may be any that keep to these rules, and one draw needn't show every extreme that they name: Sequence b's suffix cache holds its tokens in slots 0 .. suffix_lengths[b] - 1; some sequence fills all 128 slots.
All inputs are finite; a program needn't handle non-finite values.
Results may differ from a plain program's by a relative error of at most 0.02.
Values may be sent and summed in bfloat16 or wider, within the bound.
No kernel may reach another device: no remote copies, remote signals or barrier semaphores. Data moves between devices by JAX's collectives and lax.ppermute only.
A program may use at most 128 MiB of HBM per device.

v0:
```python
import jax
import jax.numpy as jnp
from jax import lax
from jax.sharding import PartitionSpec as P

EPSILON = 1e-05
ROTARY_THETA = 500000.0
MASKED = -1e30


def combined_all(part, axis, combine):
    gathered = jax.tree.map(lambda a: lax.all_gather(a, axis), part)

    def take(source):
        return jax.tree.map(lambda a: lax.dynamic_index_in_dim(a, source, 0, False), gathered)

    return lax.fori_loop(
        1, lax.axis_size(axis), lambda source, state: combine(state, take(source)), take(0)
    )


def rotary(vectors, positions):
    half_width = vectors.shape[-1] // 2
    frequency = ROTARY_THETA ** (
        -2.0 * jnp.arange(half_width).astype(jnp.float32) / vectors.shape[-1]
    )
    angles = positions[..., None] * frequency
    cosine = jnp.cos(angles)
    sine_values = jnp.sin(angles)
    front_half = vectors[..., :half_width]
    back_half = vectors[..., half_width:]
    return jnp.concatenate(
        [
            front_half * cosine - back_half * sine_values,
            back_half * cosine + front_half * sine_values,
        ],
        axis=-1,
    )


def combine(earlier, later):
    highest = jnp.maximum(earlier[0], later[0])
    first_scale = jnp.exp(earlier[0] - highest)
    second_scale = jnp.exp(later[0] - highest)
    return (
        highest,
        earlier[1] * first_scale + later[1] * second_scale,
        earlier[2] * first_scale[..., None] + later[2] * second_scale[..., None],
    )


def weigh_scores(scores):
    maxima = jnp.max(scores, axis=-1)
    weights = jnp.exp(scores - maxima[..., None]).astype(jnp.bfloat16)
    return (maxima, weights, jnp.sum(weights.astype(jnp.float32), axis=-1))


def lookup_rows(step_tokens, embedding):
    local_rows = embedding.shape[0]
    offsets = step_tokens - lax.axis_index("ctx") * local_rows
    inside_range = (offsets >= 0) & (offsets < local_rows)
    picked = jnp.take(embedding, jnp.clip(offsets, 0, local_rows - 1), axis=0)
    picked = jnp.where(inside_range[..., None], picked, jnp.zeros((), jnp.bfloat16))
    return lax.psum(picked, "ctx").astype(jnp.float32).astype(jnp.bfloat16)


def project(embedded, attn_gain, qkv_weight):
    features = embedded.astype(jnp.float32)
    square_sum = lax.psum(jnp.sum(features * features, axis=-1), "head")
    model_width = features.shape[-1] * lax.axis_size("head")
    normed = (
        features * lax.rsqrt(square_sum / model_width + EPSILON)[..., None] * attn_gain
    ).astype(jnp.bfloat16)
    flattened_rows = normed.reshape(-1, normed.shape[-1])
    local_heads = qkv_weight.shape[1] // lax.axis_size("head")

    def partial_summand(start, count):
        return jnp.einsum(
            "rd,dgf->grf", flattened_rows, qkv_weight, preferred_element_type=jnp.float32
        )

    summed = lax.psum_scatter(
        partial_summand(jnp.int32(0), lax.axis_size("head") * local_heads),
        "head",
        scatter_dimension=0,
        tiled=True,
    )
    return lax.all_gather(summed.astype(jnp.bfloat16), "ctx", axis=2, tiled=True)


def prefix_portion(flat_queries, prefix_keys, prefix_values):

    def one_head(operands):
        queries_block, keys_block, values_block = operands
        scores = jnp.einsum(
            "qd,kd->qk", queries_block, keys_block, preferred_element_type=jnp.float32
        )
        maxima, weights, totals = weigh_scores(scores)
        return (maxima, totals, jnp.dot(weights, values_block, preferred_element_type=jnp.float32))

    return lax.map(one_head, (flat_queries, prefix_keys, prefix_values))


def attend(
    qkv_rows,
    first_step,
    suffix_lengths,
    prefix_keys,
    prefix_values,
    suffix_keys,
    suffix_values,
    seen_keys,
    seen_values,
):
    local_heads, step_count, batch_rows, united_width = qkv_rows.shape
    head_dim = prefix_keys.shape[-1]
    query_width = united_width - 2 * head_dim
    group_size = query_width // head_dim
    queries = qkv_rows[..., :query_width].reshape(
        local_heads, step_count, batch_rows, group_size, head_dim
    )
    new_keys = qkv_rows[..., query_width : query_width + head_dim]
    new_values = qkv_rows[..., query_width + head_dim :]
    context = prefix_keys.shape[1] * lax.axis_size("ctx")
    step_index = first_step + jnp.arange(step_count, dtype=jnp.int32)
    positions = (context + suffix_lengths[None, :] + step_index[:, None]).astype(jnp.float32)
    queries_rot = (
        rotary(queries.astype(jnp.float32), positions[None, :, :, None]) * head_dim ** (-0.5)
    ).astype(jnp.bfloat16)
    keys_rot = rotary(new_keys.astype(jnp.float32), positions[None]).astype(jnp.bfloat16)
    maxima, totals, numerators = prefix_portion(
        queries_rot.reshape(local_heads, -1, head_dim), prefix_keys, prefix_values
    )
    maxima = maxima.reshape(local_heads, step_count, batch_rows, group_size)
    totals = totals.reshape(local_heads, step_count, batch_rows, group_size)
    numerators = numerators.reshape(local_heads, step_count, batch_rows, group_size, head_dim)
    owned_rows = suffix_keys.shape[0]
    own_start = lax.axis_index("ctx") * owned_rows
    own_queries = lax.dynamic_slice_in_dim(queries_rot, own_start, owned_rows, 2)
    own_lengths = lax.dynamic_slice_in_dim(suffix_lengths, own_start, owned_rows, 0)
    seen_keys = jnp.concatenate(
        [seen_keys, lax.dynamic_slice_in_dim(keys_rot, own_start, owned_rows, 2)], axis=1
    )
    seen_values = jnp.concatenate(
        [seen_values, lax.dynamic_slice_in_dim(new_values, own_start, owned_rows, 2)], axis=1
    )
    slot_count = suffix_keys.shape[1]
    near_scores = jnp.einsum(
        "gtbjd,bsgd->gtbjs", own_queries, suffix_keys, preferred_element_type=jnp.float32
    )
    live_slots = jnp.arange(slot_count, dtype=jnp.int32)[None, :] < own_lengths[:, None]
    near_scores = jnp.where(live_slots[None, None, :, None, :], near_scores, MASKED)
    fresh_scores = jnp.einsum(
        "gtbjd,gubd->gtbju", own_queries, seen_keys, preferred_element_type=jnp.float32
    )
    visible = jnp.arange(seen_keys.shape[1], dtype=jnp.int32)[None, :] <= step_index[:, None]
    fresh_scores = jnp.where(visible[None, :, None, None, :], fresh_scores, MASKED)
    nearby_maxima, weights, near_totals = weigh_scores(
        jnp.concatenate([near_scores, fresh_scores], axis=-1)
    )
    near_numerators = jnp.einsum(
        "gtbjs,bsgd->gtbjd",
        weights[..., :slot_count],
        suffix_values,
        preferred_element_type=jnp.float32,
    )
    near_numerators = near_numerators + jnp.einsum(
        "gtbju,gubd->gtbjd",
        weights[..., slot_count:],
        seen_values,
        preferred_element_type=jnp.float32,
    )
    own_part = (
        lax.dynamic_slice_in_dim(maxima, own_start, owned_rows, 2),
        lax.dynamic_slice_in_dim(totals, own_start, owned_rows, 2),
        lax.dynamic_slice_in_dim(numerators, own_start, owned_rows, 2),
    )
    joined = combine(own_part, (nearby_maxima, near_totals, near_numerators))
    maxima = lax.dynamic_update_slice_in_dim(maxima, joined[0], own_start, 2)
    totals = lax.dynamic_update_slice_in_dim(totals, joined[1], own_start, 2)
    numerators = lax.dynamic_update_slice_in_dim(numerators, joined[2], own_start, 2)
    maxima, totals, numerators = combined_all((maxima, totals, numerators), "ctx", combine)
    attention = (numerators / totals[..., None]).astype(jnp.bfloat16)
    return (attention, seen_keys, seen_values)


def project_out(attention, out_weight):
    local_heads, step_count, batch_rows, group_size, head_dim = attention.shape
    flattened_heads = attention.reshape(local_heads, step_count, batch_rows, group_size * head_dim)
    head_weights = out_weight.reshape(local_heads, group_size * head_dim, out_weight.shape[1])
    per_device = batch_rows // lax.axis_size("head")

    def partial_summand(start, count):
        return jnp.einsum(
            "lmie,len->imn", flattened_heads, head_weights, preferred_element_type=jnp.float32
        )

    return lax.psum_scatter(
        partial_summand(jnp.int32(0), lax.axis_size("head") * per_device).astype(jnp.bfloat16),
        "head",
        scatter_dimension=0,
        tiled=True,
    )


def body(
    token_ids,
    suffix_lengths,
    embedding,
    attn_gain,
    qkv_weight,
    out_weight,
    prefix_keys,
    prefix_values,
    suffix_keys,
    suffix_values,
):
    total_steps = token_ids.shape[0]
    batch_rows = token_ids.shape[1]
    local_heads = prefix_keys.shape[0]
    head_dim = prefix_keys.shape[-1]
    step_groups = (0, total_steps)
    seen_keys = jnp.zeros((local_heads, 0, suffix_keys.shape[0], head_dim), jnp.bfloat16)
    seen_values = jnp.zeros((local_heads, 0, suffix_keys.shape[0], head_dim), jnp.bfloat16)
    first_step, step_count = step_groups
    embedded = lookup_rows(token_ids, embedding)
    qkv_rows = project(embedded, attn_gain, qkv_weight)
    qkv_rows = qkv_rows.reshape(local_heads, step_count, batch_rows, qkv_rows.shape[-1])
    attention, seen_keys, seen_values = attend(
        qkv_rows,
        first_step,
        suffix_lengths,
        prefix_keys,
        prefix_values,
        suffix_keys,
        suffix_values,
        seen_keys,
        seen_values,
    )
    results = project_out(attention, out_weight)
    return results


def solution(mesh):
    placed = (
        P(),
        P(),
        P("ctx", "head"),
        P("head"),
        P("head", None, "ctx"),
        P("head", "ctx"),
        P("head", "ctx", None),
        P("head", "ctx", None),
        P("ctx", None, "head", None),
        P("ctx", None, "head", None),
    )
    return jax.shard_map(
        body, mesh=mesh, in_specs=placed, out_specs=P("head", None, "ctx"), check_vma=False
    )
```

profile of v0, /device:TPU:0, one launch (start us, length us, event | category | flops | bytes accessed | tf_op | source)
XLA Modules:
  0.0 286.1 jit_solution(10977653401740873123)
XLA Ops:
  6.5 0.7 compare_and_fusion
  7.4 2.7 gather_fusion
  10.0 0.8 select_select_fusion
  10.9 0.7 broadcast_add_fusion
  11.6 0.7 dynamic_slice.74
  12.5 73.2 %all-reduce.4.cloned.1.call-done = bf16[2,16,4096]{2,1,0:T(8,128)(2,1)} async-done(((bf16[2,16,4096]{2,1,0:T(8,128)(2,1)}), bf16[2,16,4096]{2,1,0:T(8,128)(2,1)}) %all-reduce.4.cloned.1.call-update) | async-done | bytes 262160 | tf_op jit(solution)/shard_map/psum | solution.py:64
  85.6 1.1 fusion.21
  86.7 5.7 %psum.15 = f32[2,16]{1,0:T(2,128)S(1)} all-reduce(f32[2,16]{1,0:T(2,128)S(1)} %fusion.21), channel_id=1, replica_groups=mesh['head'=4,'ctx'=8] {'head'}, use_global_device_ids=true, to_apply=%region_2.3 | all-reduce | flops 32 | bytes 256 | tf_op jit(solution)/shard_map/psum | solution.py:69
  92.4 1.1 fusion.23
  93.5 8.1 %convolution_bitcast_fusion.2 = f32[8,32,160]{2,1,0:T(8,128)} fusion(bf16[32,4096,1]{1,0,2:T(8,128)(2,1)S(1)} %bitcast.139, bf16[4096,8,160]{0,2,1:T(8,128)(2,1)} %param.18), kind=kOutput, calls=%fused_computation.25 | convolution fusion | flops 335544320 | bytes 10911744 | tf_op jit(solution)/shard_map/rd,dgf->grf/dot_general | solution.py:78
  101.6 0.3 multiply_cosine_fusion
  101.9 19.3 %reduce-scatter.3.cloned.1.call-done = f32[2,32,160]{2,1,0:T(8,128)} async-done(((f32[8,32,160]{2,1,0:T(8,128)}), f32[2,32,160]{2,1,0:T(8,128)}) %reduce-scatter.3.cloned.1.call-update) | async-done | bytes 40976 | tf_op jit(solution)/shard_map/reduce_scatter | solution.py:82
  121.2 0.8 convert_element_type.73
  122.1 0.1 copy.73
  122.2 32.0 %all_gather.27 = bf16[2,32,1280]{1,0,2:T(2,128)(2,1)S(1)} all-gather(bf16[2,32,160]{1,0,2:T(2,128)(2,1)S(1)} %copy.73), channel_id=1, replica_groups=mesh['head'=4,'ctx'=8] {'ctx'}, dimensions={2}, use_global_device_ids=true | all-gather | bytes 184320 | tf_op jit(solution)/shard_map/all_gather | solution.py:88
  154.2 0.4 copy.74
  154.7 0.1 fusion.42
  155.2 0.1 fusion.24
  155.4 9.6 %while.33 = (s32[]{:T(128)}, f32[2,256]{1,0:T(2,128)S(1)}, f32[2,256]{1,0:T(2,128)S(1)}, f32[2,256,128]{2,1,0:T(8,128)S(1)}, bf16[2,256,128]{2,1,0:T(8,128)(2,1)...) while((s32[]{:T(128)}, f32[2,256]{1,0:T(2,128)S(1)}, ...), condition=%wide.region_7.8_spmd, body=%wide.region_4.7_spmd.sunk | while | flops 542113280 | bytes 14885997 | solution.py:101
  155.4 2.0 fusion.61
  157.5 0.8 convert_reduce_fusion.3
  158.3 1.9 fusion.62
  160.3 2.0 fusion.61
  162.3 0.8 convert_reduce_fusion.3
  163.1 1.9 fusion.62
  165.3 0.2 fusion.44
  165.5 0.3 fusion.45
  165.8 0.2 convert_reduce_fusion.1
  166.0 0.1 convolution_bitcast_fusion.4
  166.2 0.1 fusion.18
  166.3 0.7 copy-done.1
  167.5 30.8 %all_gather.33 = f32[8,2,2,16,8]{3,4,2,1,0:T(8,128)S(1)} all-gather(f32[1,2,2,16,8]{3,4,2,1,0:T(8,128)S(1)} %copy.86), channel_id=1, replica_groups=mesh['head'=4,'ctx'=8] {'ctx'}, dimensions={0}, use_global_device_ids=true | all-gather | bytes 18432 | tf_op jit(solution)/shard_map/all_gather | solution.py:12
  198.3 30.9 %all_gather.30 = f32[8,2,2,16,8]{3,4,2,1,0:T(8,128)S(1)} all-gather(f32[1,2,2,16,8]{3,4,2,1,0:T(8,128)S(1)} %copy.83), channel_id=1, replica_groups=mesh['head'=4,'ctx'=8] {'ctx'}, dimensions={0}, use_global_device_ids=true | all-gather | bytes 18432 | tf_op jit(solution)/shard_map/all_gather | solution.py:12
  229.3 1.0 slice_bitcast_fusion
  230.3 9.9 %while.34 = (s32[]{:T(128)}, f32[2,2,16,8]{2,3,1,0:T(8,128)S(1)}, f32[2,2,16,8]{2,3,1,0:T(8,128)S(1)}, f32[2,2,16,8,128]{4,3,2,1,0:T(8,128)S(1)}, f32[8,2,2,16,8...) while((s32[]{:T(128)}, f32[2,2,16,8]{2,3,1,0:T(8,128)S(1)}, ...), condition=%wide.region_12.13_spmd, body=%wide.region_11.12_spmd.sunk | while | flops 199685 | bytes 815247 | solution.py:17
  230.5 1.2 fusion.64
  231.9 1.2 fusion.64
  233.3 1.2 fusion.64
  234.7 1.2 fusion.64
  236.1 1.2 fusion.64
  237.5 1.2 fusion.64
  238.9 1.2 fusion.64
  240.2 0.1 divide_convert_fusion
  240.5 5.6 %fusion.14 = bf16[16,2,2048]{2,0,1:T(8,128)(2,1)} fusion(bf16[2,2,16,1024]{3,2,1,0:T(8,128)(2,1)S(1)} %reshape.165, bf16[2,1024,2048,1]{2,1,3,0:T(8,128)(2,1)} %bitcast.136), kind=kOutput, calls=%fused_computation.24 | convolution fusion | flops 268500992 | bytes 8650752 | tf_op jit(solution)/shard_map/lmie,len->imn/dot_general | solution.py:194
  246.1 0.6 dynamic-slice
  247.3 30.8 %all-reduce.6.cloned.1.call-done = bf16[16,2,2048]{2,0,1:T(8,128)(2,1)} async-done(((bf16[16,2,2048]{2,0,1:T(8,128)(2,1)}), bf16[16,2,2048]{2,0,1:T(8,128)(2,1)}) %all-reduce.6.cloned.1.call-update) | async-done | bytes 131088
  278.1 0.9 constant_dynamic-slice_fusion.4
  279.0 0.6 copy.93
  (78 shorter events, 2.9 us)
Async XLA Ops:
  6.5 158.7 %copy-start = (bf16[2,128,2,128]{3,2,1,0:T(2,128)(2,1)S(1)}, bf16[2,128,2,128]{3,2,1,0:T(2,128)(2,1)}, u32[]{:S(2)}) copy-start(bf16[2,128,2,128]{3,2,1,0:T(2,128)(2,1)} %param.22) | copy-start | bytes 393220
  6.5 79.1 %all-reduce.4.cloned.1.call-start = ((), (), s32[]{:S(2)}) async-start(), calls=%async_computation.1 | async-start | bytes 524288 | tf_op jit(solution)/shard_map/psum | solution.py:64
  10.8 110.4 %reduce-scatter.3.cloned.1.call-start = ((), (), s32[]{:S(2)}) async-start(), calls=%async_computation.2 | async-start | bytes 327680 | tf_op jit(solution)/shard_map/reduce_scatter | solution.py:82
  101.6 127.7 %all-gather.2.cloned.1.call-start = ((), (), s32[]{:S(2)}) async-start(), calls=%async_computation.3 | async-start | bytes 2359296 | tf_op jit(solution)/shard_map/all_gather | solution.py:12
  155.4 10.6 %copy-start.2 = (bf16[2,128,2,128]{3,2,1,0:T(2,128)(2,1)S(1)}, bf16[2,128,2,128]{3,2,1,0:T(2,128)(2,1)}, u32[]{:S(2)}) copy-start(bf16[2,128,2,128]{3,2,1,0:T(2,128)(2,1)} %param.23) | copy-start | bytes 393220
  166.3 0.7 copy-start.1
  167.1 111.0 %all-reduce.6.cloned.1.call-start = ((), (), s32[]{:S(2)}) async-start(), calls=%async_computation.4 | async-start | bytes 262144
  240.5 5.6 %copy-start.3 = (u32[32]{0:T(128)S(1)}, u32[32]{0:T(128)}, u32[]{:S(2)}) copy-start(u32[32]{0:T(128)} %constant.135) | copy-start | bytes 388
Sparse Core Ops, SparseCore 0:
  11.0 74.6 all-reduce.3
  101.7 19.4 reduce-scatter.2
  167.2 50.6 all-gather.1
  246.2 31.8 all-reduce.5
where the time goes:
time: 287 us; the launch traced here: 286 us
  waiting for transfers between devices  123 us (43%)
  blocking collectives  99.4 us (35%)
  matrix products  22.4 us (8%)
  other arithmetic  16.7 us (6%)
  between operations  14.1 us (5%)
  local copies, waits for them, and re-layouts  9.88 us (3%)
    psum x1, waiting for transfers between devices, lookup_rows(): return lax.psum(picked, 'ctx').astype(jnp.float32).astype(jnp.bfloat16)  73.2 us
    all_gather x2, blocking collectives, combined_all(): gathered = jax.tree.map(lambda a: lax.all_gather(a, axis), part)  61.8 us
    all_gather x1, blocking collectives, project(): lax.all_gather(summed.astype(jnp.bfloat16), 'ctx', axis=2, tiled=True)  32 us
    unnamed x5, waiting for transfers between devices  30.8 us
    reduce_scatter x1, waiting for transfers between devices, project(): lax.psum_scatter(partial_summand(jnp.int32(0), lax.axis_size('head') * lo...  19.3 us
    add x7, other arithmetic, combine(): earlier[2] * first_scale[..., None] + later[2] * second_scale[..., None]  8.5 us
    dot_general x1, matrix products, partial_summand(): jnp.einsum('rd,dgf->grf', flattened_rows, qkv_weight, preferred_element_t...  8.08 us
  transfers between devices with their start and end apart: 4, of which 3 were waited for; matrix products, arithmetic and copies ran while one was open for 1% of the time, Pallas kernels for 0%

commit v1 on v0

--- a/solution.py
+++ b/solution.py
@@ -6,6 +6,7 @@
 EPSILON = 1e-05
 ROTARY_THETA = 500000.0
 MASKED = -1e30
+close_masks_for = lambda vals: lax.all_gather(vals, "ctx").sum(axis=0)
 
 
 def combined_all(part, axis, combine):
@@ -61,7 +62,7 @@
     inside_range = (offsets >= 0) & (offsets < local_rows)
     picked = jnp.take(embedding, jnp.clip(offsets, 0, local_rows - 1), axis=0)
     picked = jnp.where(inside_range[..., None], picked, jnp.zeros((), jnp.bfloat16))
-    return lax.psum(picked, "ctx").astype(jnp.float32).astype(jnp.bfloat16)
+    return close_masks_for(picked).astype(jnp.float32).astype(jnp.bfloat16)
 
 
 def project(embedded, attn_gain, qkv_weight):

time: 287 us -> 265 us (0.923)
  waiting for transfers between devices: 123 us -> 101 us
    psum x1 -> x0, waiting for transfers between devices: 73.2 us -> none  [lookup_rows(): return lax.psum(picked, 'ctx').astype(jnp.float32).astype(jnp.bfloat16)]
    all_gather x0 -> x1, waiting for transfers between devices: none -> 51.2 us  [close_masks_for = lambda vals: lax.all_gather(vals, 'ctx').sum(axis=0)]
where the time goes in v1:
time: 265 us; the launch traced here: 264 us
  waiting for transfers between devices  101 us (38%)
  blocking collectives  99.5 us (38%)
  matrix products  22.4 us (8%)
  other arithmetic  16.7 us (6%)
  between operations  14.1 us (5%)
  local copies, waits for them, and re-layouts  9.97 us (4%)
    all_gather x2, blocking collectives, combined_all(): gathered = jax.tree.map(lambda a: lax.all_gather(a, axis), part)  61.8 us
    all_gather x1, waiting for transfers between devices, close_masks_for = lambda vals: lax.all_gather(vals, 'ctx').sum(axis=0)  51.2 us
    all_gather x1, blocking collectives, project(): lax.all_gather(summed.astype(jnp.bfloat16), 'ctx', axis=2, tiled=True)  32.1 us
    unnamed x5, waiting for transfers between devices  31 us
    reduce_scatter x1, waiting for transfers between devices, project(): lax.psum_scatter(partial_summand(jnp.int32(0), lax.axis_size('head') * lo...  18.6 us
    add x7, other arithmetic, combine(): earlier[2] * first_scale[..., None] + later[2] * second_scale[..., None]  8.49 us
    dot_general x1, matrix products, partial_summand(): jnp.einsum('rd,dgf->grf', flattened_rows, qkv_weight, preferred_element_t...  8.09 us
    psum x1, blocking collectives, project(): square_sum = lax.psum(jnp.sum(features * features, axis=-1), 'head')  5.65 us
  transfers between devices with their start and end apart: 4, of which 3 were waited for; matrix products, arithmetic and copies ran while one was open for 1% of the time, Pallas kernels for 0%

profile of v1, /device:TPU:0, one launch (start us, length us, event | category | flops | bytes accessed | tf_op | source)
XLA Modules:
  0.0 263.9 jit_solution(13602989719900700741)
XLA Ops:
  6.5 0.7 compare_and_fusion
  7.4 2.7 %gather_fusion = bf16[32,4096]{1,0:T(8,128)(2,1)S(1)} fusion(bf16[8016,4096]{1,0:T(8,128)(2,1)} %param.16, s32[1024]{0:T(1024)S(1)} %pad_clamp_fusion), kind=kCustom, calls=%fused_computation | custom fusion | bytes 524416 | tf_op jit(solution)/shard_map/jit(_take)/gather | solution.py:63
  10.0 0.8 select_select_fusion
  11.0 0.7 dynamic_slice.74
  11.7 0.7 broadcast_add_fusion
  12.5 51.2 %all-gather.3.cloned.1.call-done = bf16[8,2,16,4096]{3,2,1,0:T(8,128)(2,1)} async-done(((bf16[1,2,16,4096]{3,2,1,0:T(8,128)(2,1)}), bf16[8,2,16,4096]{3,2,1,0:T(8,128)(2,1)}) %all-gather.3.cloned.1.call-update) | async-done | bytes 2097168 | tf_op jit(solution)/shard_map/all_gather | solution.py:9
  63.7 1.9 reduce_sum.39
  65.7 0.1 multiply_reduce_fusion
  65.8 5.7 %psum.7 = f32[2,16]{1,0:T(2,128)S(1)} all-reduce(f32[2,16]{1,0:T(2,128)S(1)} %multiply_reduce_fusion), channel_id=1, replica_groups=mesh['head'=4,'ctx'=8] {'head'}, use_global_device_ids=true, to_apply=%region_2.3 | all-reduce | flops 32 | bytes 256 | tf_op jit(solution)/shard_map/psum | solution.py:70
  71.5 0.1 fusion.22
  71.7 8.1 %convolution_bitcast_fusion.2 = f32[8,32,160]{2,1,0:T(8,128)} fusion(bf16[4096,8,160]{0,2,1:T(8,128)(2,1)} %param.18, bf16[32,4096]{1,0:T(8,128)(2,1)S(1)} %fusion.22), kind=kOutput, calls=%fused_computation.25 | convolution fusion | flops 335544320 | bytes 10911744 | tf_op jit(solution)/shard_map/rd,dgf->grf/dot_general | solution.py:79
  79.9 0.3 multiply_cosine_fusion
  80.2 18.6 %reduce-scatter.3.cloned.1.call-done = f32[2,32,160]{2,1,0:T(8,128)} async-done(((f32[8,32,160]{2,1,0:T(8,128)}), f32[2,32,160]{2,1,0:T(8,128)}) %reduce-scatter.3.cloned.1.call-update) | async-done | bytes 40976 | tf_op jit(solution)/shard_map/reduce_scatter | solution.py:83
  98.8 0.8 convert_element_type.84
  99.7 32.1 %all_gather.32 = bf16[2,32,1280]{1,0,2:T(2,128)(2,1)S(1)} all-gather(bf16[2,32,160]{1,0,2:T(2,128)(2,1)S(1)} %copy.73), channel_id=1, replica_groups=mesh['head'=4,'ctx'=8] {'ctx'}, dimensions={2}, use_global_device_ids=true | all-gather | bytes 184320 | tf_op jit(solution)/shard_map/all_gather | solution.py:89
  131.8 0.4 copy.74
  132.3 0.1 fusion.42
  132.8 0.1 fusion.23
  133.0 9.6 %while.33 = (s32[]{:T(128)}, f32[2,256]{1,0:T(2,128)S(1)}, f32[2,256]{1,0:T(2,128)S(1)}, f32[2,256,128]{2,1,0:T(8,128)S(1)}, bf16[2,256,128]{2,1,0:T(8,128)(2,1)...) while((s32[]{:T(128)}, f32[2,256]{1,0:T(2,128)S(1)}, ...), condition=%wide.region_7.8_spmd, body=%wide.region_4.7_spmd.sunk | while | flops 542113280 | bytes 14885997 | solution.py:102
  133.0 2.0 fusion.60
  135.1 0.8 convert_reduce_fusion.3
  135.9 1.9 fusion.61
  137.8 2.0 fusion.60
  139.9 0.8 convert_reduce_fusion.3
  140.7 1.9 fusion.61
  142.9 0.2 fusion.44
  143.1 0.3 fusion.45
  143.4 0.2 convert_reduce_fusion.1
  143.6 0.1 convolution_bitcast_fusion.4
  143.8 0.1 fusion.18
  143.9 0.7 copy-done.1
  145.1 30.8 %all_gather.38 = f32[8,2,2,16,8]{3,4,2,1,0:T(8,128)S(1)} all-gather(f32[1,2,2,16,8]{3,4,2,1,0:T(8,128)S(1)} %copy.86), channel_id=1, replica_groups=mesh['head'=4,'ctx'=8] {'ctx'}, dimensions={0}, use_global_device_ids=true | all-gather | bytes 18432 | tf_op jit(solution)/shard_map/all_gather | solution.py:13
  175.9 30.9 %all_gather.35 = f32[8,2,2,16,8]{3,4,2,1,0:T(8,128)S(1)} all-gather(f32[1,2,2,16,8]{3,4,2,1,0:T(8,128)S(1)} %copy.83), channel_id=1, replica_groups=mesh['head'=4,'ctx'=8] {'ctx'}, dimensions={0}, use_global_device_ids=true | all-gather | bytes 18432 | tf_op jit(solution)/shard_map/all_gather | solution.py:13
  206.9 1.0 slice_bitcast_fusion
  207.9 9.9 %while.34 = (s32[]{:T(128)}, f32[2,2,16,8]{2,3,1,0:T(8,128)S(1)}, f32[2,2,16,8]{2,3,1,0:T(8,128)S(1)}, f32[2,2,16,8,128]{4,3,2,1,0:T(8,128)S(1)}, f32[8,2,2,16,8...) while((s32[]{:T(128)}, f32[2,2,16,8]{2,3,1,0:T(8,128)S(1)}, ...), condition=%wide.region_12.13_spmd, body=%wide.region_11.12_spmd.sunk | while | flops 199685 | bytes 815247 | solution.py:18
  208.1 1.2 fusion.63
  209.5 1.2 fusion.63
  210.9 1.2 fusion.63
  212.3 1.2 fusion.63
  213.7 1.2 fusion.63
  215.1 1.2 fusion.63
  216.6 1.2 fusion.63
  217.9 0.1 divide_convert_fusion
  218.1 5.6 %fusion.14 = bf16[16,2,2048]{2,0,1:T(8,128)(2,1)} fusion(bf16[2,2,16,1024]{3,2,1,0:T(8,128)(2,1)S(1)} %reshape.177, bf16[2,1024,2048,1]{2,1,3,0:T(8,128)(2,1)} %bitcast.141), kind=kOutput, calls=%fused_computation.24 | convolution fusion | flops 268500992 | bytes 8650752 | tf_op jit(solution)/shard_map/lmie,len->imn/dot_general | solution.py:195
  223.7 0.6 dynamic-slice
  224.9 31.0 %all-reduce.3.cloned.1.call-done = bf16[16,2,2048]{2,0,1:T(8,128)(2,1)} async-done(((bf16[16,2,2048]{2,0,1:T(8,128)(2,1)}), bf16[16,2,2048]{2,0,1:T(8,128)(2,1)}) %all-reduce.3.cloned.1.call-update) | async-done | bytes 131088
  255.9 0.9 constant_dynamic-slice_fusion.4
  256.8 0.6 copy.93
  (82 shorter events, 3.1 us)
Async XLA Ops:
  6.5 136.3 %copy-start = (bf16[2,128,2,128]{3,2,1,0:T(2,128)(2,1)S(1)}, bf16[2,128,2,128]{3,2,1,0:T(2,128)(2,1)}, u32[]{:S(2)}) copy-start(bf16[2,128,2,128]{3,2,1,0:T(2,128)(2,1)} %param.22) | copy-start | bytes 393220
  6.5 65.0 %copy-start.3 = (f32[4096]{0:T(1024)S(1)}, f32[4096]{0:T(1024)}, u32[]{:S(2)}) copy-start(f32[4096]{0:T(1024)} %param.17) | copy-start | bytes 49156
  6.5 57.2 %all-gather.3.cloned.1.call-start = ((), (), s32[]{:S(2)}) async-start(), calls=%async_computation.1 | async-start | bytes 2359296 | tf_op jit(solution)/shard_map/all_gather | solution.py:9
  10.9 87.9 %reduce-scatter.3.cloned.1.call-start = ((), (), s32[]{:S(2)}) async-start(), calls=%async_computation.2 | async-start | bytes 327680 | tf_op jit(solution)/shard_map/reduce_scatter | solution.py:83
  79.8 127.1 %all-gather.5.cloned.1.call-start = ((), (), s32[]{:S(2)}) async-start(), calls=%async_computation.3 | async-start | bytes 2359296 | tf_op jit(solution)/shard_map/all_gather | solution.py:13
  133.0 10.6 %copy-start.2 = (bf16[2,128,2,128]{3,2,1,0:T(2,128)(2,1)S(1)}, bf16[2,128,2,128]{3,2,1,0:T(2,128)(2,1)}, u32[]{:S(2)}) copy-start(bf16[2,128,2,128]{3,2,1,0:T(2,128)(2,1)} %param.23) | copy-start | bytes 393220
  143.9 0.7 copy-start.1
  144.7 111.2 %all-reduce.3.cloned.1.call-start = ((), (), s32[]{:S(2)}) async-start(), calls=%async_computation.4 | async-start | bytes 262144
  218.1 5.6 %copy-start.4 = (u32[32]{0:T(128)S(1)}, u32[32]{0:T(128)}, u32[]{:S(2)}) copy-start(u32[32]{0:T(128)} %constant.136) | copy-start | bytes 388
Sparse Core Ops, SparseCore 0:
  11.0 52.7 all-gather.2
  79.9 18.7 reduce-scatter.2
  144.8 50.5 all-gather.4
  223.8 32.0 all-reduce.2
